TPU v7x, 32 devices: a whole 2x2x4 slice. The times are simulated.
32 devices in a mesh: region: 8 (over z, x), tm: 4 (over y, core).
Axes of the slice: x: 2, y: 2, z: 4, core: 2. Of those that a mesh axis runs over, the one named last changes fastest.
Arguments:
- observations: bfloat16 [8, 4, 2048, 512], P('region', 'tm'), may hold values from -160 to 160
- counts: int32 [8, 4], P('region', 'tm'), may hold values from 1 to 8, as said below
- visible: int32 [8, 8], replicated, may hold values 0 or 1
- latents: bfloat16 [8, 32, 512], P('region'), may hold values from -6 to 6
- lat_gain: float32 [512], replicated, may hold values from 0.5 to 1.5
- mlp_gain: float32 [512], replicated, may hold values from 0.5 to 1.5
- w_query: bfloat16 [512, 512], replicated, may hold values from -0.25 to 0.25
- w_keyval: bfloat16 [512, 1024], replicated, may hold values from -0.25 to 0.25
- w_out: bfloat16 [512, 512], replicated, may hold values from -0.25 to 0.25
- w_up: bfloat16 [512, 2048], P(None, 'tm'), may hold values from -0.25 to 0.25
- w_down: bfloat16 [2048, 512], P('tm'), may hold values from -0.125 to 0.125
Outputs:
- encoded: bfloat16 [8, 32, 512], P('region')
Inputs may be any that keep to these rules, and one draw needn't show every extreme that they name: `counts`: some region and time slot holds 8 blocks.
All inputs are finite; a program needn't handle non-finite values.
Results may differ from a plain program's by a relative error of at most 0.0055.
The roundings to bfloat16 on the way count: a program that leaves them out, or rounds other values in their place, can miss the bound.
Values may be sent and summed in bfloat16 or wider, within the bound.
A program may use at most 64 MiB of HBM per device.

v0:
```python
import math
import jax
import jax.numpy as jnp
from jax import lax
from jax.sharding import PartitionSpec as P

H = 8
BLK = 256
NEG = -1e30


def joined(x, axis, combine):
    everything = jax.tree.map(lambda part: lax.all_gather(part, axis), x)
    leading = jax.tree.map(lambda part: part[0], everything)

    def step(k, so_far):
        return combine(so_far, jax.tree.map(lambda part: part[k], everything))

    return lax.fori_loop(1, lax.axis_size(axis), step, leading)


def layer_norm(values, gain):
    average = jnp.mean(values, axis=-1, keepdims=True)
    centered = values - average
    variance = jnp.mean(centered * centered, axis=-1, keepdims=True)
    return centered * lax.rsqrt(variance + 1e-05) * gain


def expand(factor, model_width):
    return jnp.repeat(factor, model_width // factor.shape[-1], axis=-1)


def combine(first, second):
    first_num, first_den, first_peak = first
    second_num, second_den, second_peak = second
    highest = jnp.maximum(first_peak, second_peak)
    first_scale = jnp.exp(first_peak - highest)
    second_scale = jnp.exp(second_peak - highest)
    numerator = first_num * expand(first_scale, first_num.shape[-1]) + second_num * expand(
        second_scale, second_num.shape[-1]
    )
    return (numerator, first_den * first_scale + second_den * second_scale, highest)


def partials(query_rows, key_heads, value_heads, allowed, head_size):
    row_count = query_rows.shape[0]
    query_heads = query_rows.reshape(row_count, H, head_size)
    scores = jnp.einsum(
        "qhd,khd->hqk", query_heads, key_heads, preferred_element_type=jnp.float32
    ) * head_size ** (-0.5)
    scores = jnp.where(allowed[None], scores, NEG)
    peaks = jnp.max(scores, axis=-1)
    weights = jnp.where(allowed[None], jnp.exp(scores - peaks[..., None]), 0.0)
    denominator = jnp.sum(weights, axis=-1)
    numerator = jnp.einsum(
        "hqk,khd->qhd",
        weights.astype(jnp.bfloat16),
        value_heads,
        preferred_element_type=jnp.float32,
    )
    return (numerator.reshape(row_count, H * head_size), denominator.T, peaks.T)


def on_device(
    observations,
    counts,
    visible,
    latents,
    lat_gain,
    mlp_gain,
    w_query,
    w_keyval,
    w_out,
    w_up,
    w_down,
):
    regions = lax.axis_size("region")
    own_region = lax.axis_index("region")
    latent_rows = latents.shape[1]
    model_width = latents.shape[2]
    head_size = model_width // H
    observed = observations[0, 0]
    obs_rows = observed.shape[0]
    latent_state = latents[0].astype(jnp.float32)
    normed = layer_norm(latent_state, lat_gain).astype(jnp.bfloat16)
    own_queries = jnp.dot(normed, w_query, preferred_element_type=jnp.float32).astype(jnp.bfloat16)
    every_query = lax.all_gather(own_queries, "region", axis=0, tiled=True)
    keyval = jnp.dot(observed, w_keyval, preferred_element_type=jnp.float32).astype(jnp.bfloat16)
    key_heads = keyval[:, :model_width].reshape(obs_rows, H, head_size)
    value_heads = keyval[:, model_width:].reshape(obs_rows, H, head_size)
    live_rows = lax.iota(jnp.int32, obs_rows) < counts[0, 0] * BLK
    column = lax.dynamic_slice_in_dim(visible, own_region, 1, 1)[:, 0]
    sees_source = (column > 0) | (lax.iota(jnp.int32, regions) == own_region)
    per_block = math.gcd(regions, max(1, 256 // latent_rows))
    block_count = regions // per_block
    query_blocks = every_query.reshape(block_count, per_block * latent_rows, model_width)
    sees_blocks = jnp.repeat(sees_source, latent_rows).reshape(block_count, per_block * latent_rows)

    def one_block(operands):
        query_rows, sees_rows = operands
        allowed = sees_rows[:, None] & live_rows[None, :]
        return partials(query_rows, key_heads, value_heads, allowed, head_size)

    numerators, denominators, peaks = lax.map(one_block, (query_blocks, sees_blocks))
    numerators = numerators.reshape(regions, latent_rows, model_width)
    denominators = denominators.reshape(regions, latent_rows, H)
    peaks = peaks.reshape(regions, latent_rows, H)
    got_num, got_den, got_peak = (
        lax.all_to_all(numerators, "region", split_axis=0, concat_axis=0, tiled=True),
        lax.all_to_all(denominators, "region", split_axis=0, concat_axis=0, tiled=True),
        lax.all_to_all(peaks, "region", split_axis=0, concat_axis=0, tiled=True),
    )
    highest = jnp.max(got_peak, axis=0)
    factor = jnp.exp(got_peak - highest[None])
    numerator = jnp.sum(got_num * expand(factor, model_width), axis=0)
    denominator = jnp.sum(got_den * factor, axis=0)
    numerator, denominator, highest = joined((numerator, denominator, highest), "tm", combine)
    attended = (numerator / expand(denominator, model_width)).astype(jnp.bfloat16)
    residual = latent_state + jnp.dot(attended, w_out, preferred_element_type=jnp.float32)
    normed2 = layer_norm(residual, mlp_gain).astype(jnp.bfloat16)
    hidden = jax.nn.gelu(
        jnp.dot(normed2, w_up, preferred_element_type=jnp.float32), approximate=True
    ).astype(jnp.bfloat16)
    mlp_part = jnp.dot(hidden, w_down, preferred_element_type=jnp.float32)
    mlp_total = lax.psum(mlp_part, "tm")
    return (residual + mlp_total).astype(jnp.bfloat16)[None]


def solution(mesh):
    placed = (
        P("region", "tm", None, None),
        P("region", "tm"),
        P(),
        P("region", None, None),
        P(),
        P(),
        P(),
        P(),
        P(),
        P(None, "tm"),
        P("tm", None),
    )
    return jax.shard_map(
        on_device, mesh=mesh, in_specs=placed, out_specs=P("region", None, None), check_vma=False
    )
```

profile of v0, /device:TPU:0, one launch (start us, length us, event | category | flops | bytes accessed | tf_op | source)
XLA Modules:
  0.0 166.7 jit_solution(793247751511443457)
XLA Ops:
  10.2 1.3 convolution_convert_fusion.1
  11.5 32.6 %all_gather.19 = bf16[256,512]{1,0:T(8,128)(2,1)S(1)} all-gather(bf16[32,512]{1,0:T(8,128)(2,1)S(1)} %convolution_convert_fusion.1), channel_id=1, replica_groups=mesh['region'=8,'tm'=4] {'region'}, dimensions={0}, use_global_device_ids=true | all-gather | bytes 294912 | tf_op jit(solution)/shard_map/all_gather | solution.py:87
  44.3 3.6 %convolution_convert_fusion = bf16[2048,1024]{0,1:T(8,128)(2,1)S(1)} fusion(bf16[512,1024]{1,0:T(8,128)(2,1)} %param.20, bf16[1,1,2048,512]{3,2,1,0:T(8,128)(2,1)S(1)} %copy-done), kind=kOutput, calls=%fused_computation.17 | convolution fusion | flops 2149580800 | bytes 7340032 | tf_op jit(solution)/shard_map/dot_general | solution.py:88
  47.9 1.8 %fusion.53 = (bf16[2048,512]{0,1:T(8,128)(2,1)S(1)}, bf16[2048,512]{0,1:T(8,128)(2,1)}) fusion(bf16[2048,1024]{0,1:T(8,128)(2,1)S(1)} %convolution_convert_fusion), kind=kLoop, calls=%fused_computation.77 | loop fusion | bytes 8388608 | tf_op jit(solution)/shard_map/slice | solution.py:89
  50.0 3.2 %fusion.3 = (f32[8,256]{1,0:T(8,128)S(1)}, f32[8,256,2048]{2,1,0:T(8,128)S(1)}) fusion(pred[256,2048]{1,0:T(8,128)(4,1)S(1)} %broadcast_and_fusion, bf16[256,8,64]{0,2,1:T(8,128)(2,1)S(1)} %bitcast.84, bf16[2048,8,64]{0,2,1:T(8,128)(2,1)S(1)} %bitcast.81), kind=kOutput, calls=%fused_computation.12 | convolution fusion | flops 549451776 | bytes 19668992 | tf_op jit(solution)/shard_map/while/body/eval_jaxpr/qhd,khd->hqk/dot_general | solution.py:48
  53.2 5.7 %copy-done.1 = f32[8,256,2048]{2,1,0:T(8,128)} copy-done((f32[8,256,2048]{2,1,0:T(8,128)}, f32[8,256,2048]{2,1,0:T(8,128)S(1)}, u32[]{:S(2)}) %copy-start.1) | copy-done | bytes 16777240
  58.9 5.0 %fusion.4 = f32[8,256]{1,0:T(8,128)S(1)} fusion(f32[8,256,2048]{2,1,0:T(8,128)S(1)} %get-tuple-element.250, f32[8,256]{1,0:T(8,128)S(1)} %get-tuple-element.249, pred[256,2048]{1,0:T(8,128)(4,1)S(1)} %broadcast_and_fusion), kind=kLoop, calls=%fused_computation.13 | loop fusion | flops 20969472 | bytes 17317888 | tf_op jit(solution)/shard_map/while/body/eval_jaxpr/reduce_sum | solution.py:54
  64.6 5.5 %all-to-all-start.2 = ((f32[8,1,256]{2,1,0:T(1,128)}), f32[8,1,256]{2,1,0:T(1,128)S(1)}, u32[]{:S(2)}, u32[]{:S(2)}) async-start(f32[8,1,256]{2,1,0:T(1,128)} %reshape.151), calls=%async_computation.2 | async-start | bytes 16384 | tf_op jit(solution)/shard_map/all_to_all | solution.py:110
  70.9 5.8 %all-to-all-done.2 = f32[8,1,256]{2,1,0:T(1,128)S(1)} async-done(((f32[8,1,256]{2,1,0:T(1,128)}), f32[8,1,256]{2,1,0:T(1,128)S(1)}, u32[]{:S(2)}, u32[]{:S(2)}) %all-to-all-start.2) | async-done | bytes 8224 | tf_op jit(solution)/shard_map/all_to_all | solution.py:110
  76.7 3.3 %all-to-all-start.1 = ((f32[8,1,256]{2,1,0:T(1,128)}), f32[8,1,256]{2,1,0:T(1,128)S(1)}, u32[]{:S(2)}, u32[]{:S(2)}) async-start(f32[8,1,256]{2,1,0:T(1,128)} %reshape.149), calls=%async_computation.1 | async-start | bytes 16384 | tf_op jit(solution)/shard_map/all_to_all | solution.py:111
  80.0 9.4 %fusion.10 = f32[256,8,64]{0,2,1:T(8,128)} fusion(bf16[2048,8,64]{0,2,1:T(8,128)(2,1)} %bitcast.82, f32[8,256,2048]{2,1,0:T(8,128)} %copy-done.1, f32[8,256]{1,0:T(8,128)S(1)} %get-tuple-element.249, pred[256,2048]{1,0:T(8,128)(4,1)S(1)} %broadcast_and_fusion), kind=kOutput, calls=%fused_computation.19 | convolution fusion | flops 557842432 | bytes 19931136 | tf_op jit(solution)/shard_map/while/body/eval_jaxpr/hqk,khd->qhd/dot_general | solution.py:55
  89.4 1.5 copy.28
  90.9 1.1 reshape.126
  92.0 5.9 %all-to-all-start = ((f32[8,32,512]{2,1,0:T(8,128)}), f32[8,32,512]{2,1,0:T(8,128)}, u32[]{:S(2)}, u32[]{:S(2)}) async-start(f32[8,32,512]{2,1,0:T(8,128)} %reshape.126), calls=%async_computation | async-start | bytes 1048576 | tf_op jit(solution)/shard_map/all_to_all | solution.py:109
  100.6 1.1 reshape.128
  101.7 5.2 %all-gather.3 = f32[4,32,8]{1,2,0:T(8,128)S(1)} all-gather(f32[1,32,8]{1,2,0:T(8,128)S(1)} %bitcast.90), channel_id=3, replica_groups=mesh['region'=8,'tm'=4] {'tm'}, dimensions={0}, use_global_device_ids=true | all-gather | bytes 5120 | tf_op jit(solution)/shard_map/all_gather | solution.py:13
  107.0 5.2 %all-gather.4 = f32[4,32,8]{1,2,0:T(8,128)S(1)} all-gather(f32[1,32,8]{1,2,0:T(8,128)S(1)} %bitcast.88), channel_id=4, replica_groups=mesh['region'=8,'tm'=4] {'tm'}, dimensions={0}, use_global_device_ids=true | all-gather | bytes 5120 | tf_op jit(solution)/shard_map/all_gather | solution.py:13
  112.2 1.3 multiply_reduce_fusion
  113.5 5.8 %all-gather = f32[128,512]{1,0:T(8,128)S(1)} all-gather(f32[32,512]{1,0:T(8,128)S(1)} %multiply_reduce_fusion), channel_id=2, replica_groups=mesh['region'=8,'tm'=4] {'tm'}, dimensions={0}, use_global_device_ids=true | all-gather | bytes 327680 | tf_op jit(solution)/shard_map/all_gather | solution.py:13
  119.4 1.9 %while.12 = (s32[]{:T(128)}, f32[32,512]{1,0:T(8,128)S(1)}, f32[32,8]{1,0:T(8,128)S(1)}, f32[32,8]{1,0:T(8,128)S(1)}, f32[4,32,8]{1,2,0:T(8,128)S(1)}, /*index=5...) while((s32[]{:T(128)}, f32[32,512]{1,0:T(8,128)S(1)}, ...), condition=%wide.region_8.9_spmd, body=%wide.region_7.8_spmd.sunk | while | flops 50693 | bytes 739479 | solution.py:19
  121.5 1.3 fusion.54
  123.0 2.2 %fusion.28 = f32[32,512]{1,0:T(8,128)} fusion(bf16[512,512]{1,0:T(8,128)(2,1)} %param.23, bf16[512,512]{1,0:T(8,128)(2,1)} %param.22, f32[32,512]{1,0:T(8,128)S(1)} %get-tuple-element.252, f32[512]{0:T(512)S(1)} %copy-done.3, f32[32]{0:T(128)S(1)} %add_rsqrt_fusion, f32[32]{0:T(128)S(1)} %broadcast_multiply_fusion), kind=kOutput, calls=%fused_computation.46 | convolution fusion | flops 33767424 | bytes 1181952 | tf_op jit(solution)/shard_map/dot_general | solution.py:124
  125.3 33.1 %all-reduce.2.cloned.1.call-done = f32[32,512]{1,0:T(8,128)} async-done(((f32[32,512]{1,0:T(8,128)}), f32[32,512]{1,0:T(8,128)}) %all-reduce.2.cloned.1.call-update) | async-done | bytes 65552 | tf_op jit(solution)/shard_map/psum | solution.py:125
  158.4 1.5 fusion.29
  (74 shorter events, 10.0 us)
Async XLA Ops:
  6.5 37.7 %copy-start = (bf16[1,1,2048,512]{3,2,1,0:T(8,128)(2,1)S(1)}, bf16[1,1,2048,512]{3,2,1,0:T(8,128)(2,1)}, u32[]{:S(2)}) copy-start(bf16[1,1,2048,512]{3,2,1,0:T(8,128)(2,1)} %param.13) | copy-start | bytes 6291460
  53.2 5.7 %copy-start.1 = (f32[8,256,2048]{2,1,0:T(8,128)}, f32[8,256,2048]{2,1,0:T(8,128)S(1)}, u32[]{:S(2)}) copy-start(f32[8,256,2048]{2,1,0:T(8,128)S(1)} %get-tuple-element.250) | copy-start | bytes 50331652
  64.6 12.0 %all-to-all-start.2 = ((f32[8,1,256]{2,1,0:T(1,128)}), f32[8,1,256]{2,1,0:T(1,128)S(1)}, u32[]{:S(2)}, u32[]{:S(2)}) async-start(f32[8,1,256]{2,1,0:T(1,128)} %reshape.151), calls=%async_computation.2 | async-start | bytes 16384 | tf_op jit(solution)/shard_map/all_to_all | solution.py:110
  76.7 15.3 %all-to-all-start.1 = ((f32[8,1,256]{2,1,0:T(1,128)}), f32[8,1,256]{2,1,0:T(1,128)S(1)}, u32[]{:S(2)}, u32[]{:S(2)}) async-start(f32[8,1,256]{2,1,0:T(1,128)} %reshape.149), calls=%async_computation.1 | async-start | bytes 16384 | tf_op jit(solution)/shard_map/all_to_all | solution.py:111
  80.0 41.5 %copy-start.2 = (bf16[1,32,512]{2,1,0:T(8,128)(2,1)S(1)}, bf16[1,32,512]{2,1,0:T(8,128)(2,1)}, u32[]{:S(2)}) copy-start(bf16[1,32,512]{2,1,0:T(8,128)(2,1)} %param.16) | copy-start | bytes 98308
  80.0 43.0 %copy-start.3 = (f32[512]{0:T(512)S(1)}, f32[512]{0:T(512)}, u32[]{:S(2)}) copy-start(f32[512]{0:T(512)} %param.18) | copy-start | bytes 6148
  92.0 20.3 %all-to-all-start = ((f32[8,32,512]{2,1,0:T(8,128)}), f32[8,32,512]{2,1,0:T(8,128)}, u32[]{:S(2)}, u32[]{:S(2)}) async-start(f32[8,32,512]{2,1,0:T(8,128)} %reshape.126), calls=%async_computation | async-start | bytes 1048576 | tf_op jit(solution)/shard_map/all_to_all | solution.py:109
  97.9 60.5 %all-reduce.2.cloned.1.call-start = ((), (), s32[]{:S(2)}) async-start(), calls=%async_computation.3 | async-start | bytes 131072 | tf_op jit(solution)/shard_map/psum | solution.py:125
Sparse Core Ops, SparseCore 0:
  125.4 32.9 all-reduce.1
where the time goes:
time: 167 us
  blocking collectives  48.8 us (29%)
  waiting for transfers between devices  38.9 us (23%)
  matrix products  21.1 us (13%)
  local copies, waits for them, and re-layouts  16.1 us (10%)
  starting transfers between devices  14.8 us (9%)
  between operations  14.2 us (9%)
  other arithmetic  12.7 us (8%)
    psum x1, waiting for transfers between devices, on_device(): mlp_total = lax.psum(mlp_part, 'tm')  33.1 us
    all_gather x1, blocking collectives, on_device(): every_query = lax.all_gather(own_queries, 'region', axis=0, tiled=True)  32.6 us
    all_gather x3, blocking collectives, joined(): everything = jax.tree.map(lambda part: lax.all_gather(part, axis), x)  16.2 us
    dot_general x1, matrix products, partials(): jnp.einsum('hqk,khd->qhd', weights.astype(jnp.bfloat16), value_heads, pre...  9.39 us
    unnamed x12, local copies, waits for them, and re-layouts  7.23 us
    all_to_all x1, starting transfers between devices, on_device(): lax.all_to_all(numerators, 'region', split_axis=0, concat_axis=0, tiled=T...  5.93 us
    all_to_all x1, waiting for transfers between devices, on_device(): lax.all_to_all(denominators, 'region', split_axis=0, concat_axis=0, tiled...  5.75 us
    all_to_all x1, starting transfers between devices, on_device(): lax.all_to_all(denominators, 'region', split_axis=0, concat_axis=0, tiled...  5.52 us
  transfers between devices with their start and end apart: 4, of which 2 were waited for; matrix products, arithmetic and copies ran while one was open for 10% of the time, Pallas kernels for 0%

commit v1 on v0

--- a/solution.py
+++ b/solution.py
@@ -7,6 +7,11 @@
 H = 8
 BLK = 256
 NEG = -1e30
+
+
+def summed_here(x, name):
+    terms = lax.all_gather(x, name)
+    return jnp.sum(terms, axis=0)
 
 
 def joined(x, axis, combine):
@@ -122,7 +127,7 @@
         jnp.dot(normed2, w_up, preferred_element_type=jnp.float32), approximate=True
     ).astype(jnp.bfloat16)
     mlp_part = jnp.dot(hidden, w_down, preferred_element_type=jnp.float32)
-    mlp_total = lax.psum(mlp_part, "tm")
+    mlp_total = summed_here(mlp_part, "tm")
     return (residual + mlp_total).astype(jnp.bfloat16)[None]
 
 

time: 167 us -> 125 us (0.75)
  waiting for transfers between devices: 38.9 us -> 5.76 us
  between operations: 14.2 us -> 0.86 us
  blocking collectives: 48.8 us -> 54.6 us
    psum x1 -> x0, waiting for transfers between devices: 33.1 us -> none  [on_device(): mlp_total = lax.psum(mlp_part, 'tm')]
    all_gather x0 -> x1, blocking collectives: none -> 5.85 us  [summed_here(): terms = lax.all_gather(x, name)]
  transfers between devices with their start and end apart: 4 -> 3, of which waited for: 2 -> 1; matrix products, arithmetic and copies ran while one was open for 10% -> 13% of each run, Pallas kernels for 0% -> 0%
where the time goes in v1:
time: 125 us
  blocking collectives  54.6 us (44%)
  matrix products  20.4 us (16%)
  local copies, waits for them, and re-layouts  16.1 us (13%)
  starting transfers between devices  14.8 us (12%)
  other arithmetic  11.9 us (10%)
  waiting for transfers between devices  5.76 us (5%)
    all_gather x1, blocking collectives, on_device(): every_query = lax.all_gather(own_queries, 'region', axis=0, tiled=True)  32.6 us
    all_gather x3, blocking collectives, joined(): everything = jax.tree.map(lambda part: lax.all_gather(part, axis), x)  16.2 us
    dot_general x1, matrix products, partials(): jnp.einsum('hqk,khd->qhd', weights.astype(jnp.bfloat16), value_heads, pre...  9.39 us
    unnamed x12, local copies, waits for them, and re-layouts  7.23 us
    all_to_all x1, starting transfers between devices, on_device(): lax.all_to_all(numerators, 'region', split_axis=0, concat_axis=0, tiled=T...  5.93 us
    all_gather x1, blocking collectives, summed_here(): terms = lax.all_gather(x, name)  5.85 us
    all_to_all x1, waiting for transfers between devices, on_device(): lax.all_to_all(denominators, 'region', split_axis=0, concat_axis=0, tiled...  5.75 us
    all_to_all x1, starting transfers between devices, on_device(): lax.all_to_all(denominators, 'region', split_axis=0, concat_axis=0, tiled...  5.52 us
  transfers between devices with their start and end apart: 3, of which 1 were waited for; matrix products, arithmetic and copies ran while one was open for 13% of the time, Pallas kernels for 0%

profile of v1, /device:TPU:0, one launch (start us, length us, event | category | flops | bytes accessed | tf_op | source)
XLA Modules:
  0.0 124.6 jit_solution(2754602983105251853)
XLA Ops:
  0.0 1.0 fusion.44
  3.7 1.3 %convolution_convert_fusion.1 = bf16[32,512]{1,0:T(8,128)(2,1)S(1)} fusion(bf16[512,512]{1,0:T(8,128)(2,1)} %param.19, bf16[1,32,512]{2,1,0:T(8,128)(2,1)} %param.16, f32[512]{0:T(512)} %param.17, f32[32]{0:T(128)S(1)} %add_rsqrt_fusion.1, f32[32]{0:T(128)S(1)} %broadcast_multiply_fusion.1), kind=kOutput, calls=%fused_computation.21 | convolution fusion | flops 16875520 | bytes 592128 | tf_op jit(solution)/shard_map/dot_general | solution.py:91
  5.0 32.6 %all_gather.25 = bf16[256,512]{1,0:T(8,128)(2,1)S(1)} all-gather(bf16[32,512]{1,0:T(8,128)(2,1)S(1)} %convolution_convert_fusion.1), channel_id=1, replica_groups=mesh['region'=8,'tm'=4] {'region'}, dimensions={0}, use_global_device_ids=true | all-gather | bytes 294912 | tf_op jit(solution)/shard_map/all_gather | solution.py:92
  37.7 3.6 %convolution_convert_fusion = bf16[2048,1024]{0,1:T(8,128)(2,1)S(1)} fusion(bf16[512,1024]{1,0:T(8,128)(2,1)} %param.20, bf16[1,1,2048,512]{3,2,1,0:T(8,128)(2,1)S(1)} %copy-done), kind=kOutput, calls=%fused_computation.17 | convolution fusion | flops 2149580800 | bytes 7340032 | tf_op jit(solution)/shard_map/dot_general | solution.py:93
  41.3 1.8 %fusion.53 = (bf16[2048,512]{0,1:T(8,128)(2,1)S(1)}, bf16[2048,512]{0,1:T(8,128)(2,1)}) fusion(bf16[2048,1024]{0,1:T(8,128)(2,1)S(1)} %convolution_convert_fusion), kind=kLoop, calls=%fused_computation.77 | loop fusion | bytes 8388608 | tf_op jit(solution)/shard_map/slice | solution.py:94
  43.4 3.2 %fusion.3 = (f32[8,256]{1,0:T(8,128)S(1)}, f32[8,256,2048]{2,1,0:T(8,128)S(1)}) fusion(pred[256,2048]{1,0:T(8,128)(4,1)S(1)} %broadcast_and_fusion, bf16[256,8,64]{0,2,1:T(8,128)(2,1)S(1)} %bitcast.85, bf16[2048,8,64]{0,2,1:T(8,128)(2,1)S(1)} %bitcast.82), kind=kOutput, calls=%fused_computation.12 | convolution fusion | flops 549451776 | bytes 19668992 | tf_op jit(solution)/shard_map/while/body/eval_jaxpr/qhd,khd->hqk/dot_general | solution.py:53
  46.6 5.7 %copy-done.1 = f32[8,256,2048]{2,1,0:T(8,128)} copy-done((f32[8,256,2048]{2,1,0:T(8,128)}, f32[8,256,2048]{2,1,0:T(8,128)S(1)}, u32[]{:S(2)}) %copy-start.1) | copy-done | bytes 16777240
  52.4 5.0 %fusion.4 = f32[8,256]{1,0:T(8,128)S(1)} fusion(f32[8,256,2048]{2,1,0:T(8,128)S(1)} %get-tuple-element.250, f32[8,256]{1,0:T(8,128)S(1)} %get-tuple-element.249, pred[256,2048]{1,0:T(8,128)(4,1)S(1)} %broadcast_and_fusion), kind=kLoop, calls=%fused_computation.13 | loop fusion | flops 20969472 | bytes 17317888 | tf_op jit(solution)/shard_map/while/body/eval_jaxpr/reduce_sum | solution.py:59
  58.1 5.5 %all-to-all-start.2 = ((f32[8,1,256]{2,1,0:T(1,128)}), f32[8,1,256]{2,1,0:T(1,128)S(1)}, u32[]{:S(2)}, u32[]{:S(2)}) async-start(f32[8,1,256]{2,1,0:T(1,128)} %reshape.152), calls=%async_computation.2 | async-start | bytes 16384 | tf_op jit(solution)/shard_map/all_to_all | solution.py:115
  64.4 5.8 %all-to-all-done.2 = f32[8,1,256]{2,1,0:T(1,128)S(1)} async-done(((f32[8,1,256]{2,1,0:T(1,128)}), f32[8,1,256]{2,1,0:T(1,128)S(1)}, u32[]{:S(2)}, u32[]{:S(2)}) %all-to-all-start.2) | async-done | bytes 8224 | tf_op jit(solution)/shard_map/all_to_all | solution.py:115
  70.1 3.3 %all-to-all-start.1 = ((f32[8,1,256]{2,1,0:T(1,128)}), f32[8,1,256]{2,1,0:T(1,128)S(1)}, u32[]{:S(2)}, u32[]{:S(2)}) async-start(f32[8,1,256]{2,1,0:T(1,128)} %reshape.150), calls=%async_computation.1 | async-start | bytes 16384 | tf_op jit(solution)/shard_map/all_to_all | solution.py:116
  73.5 9.4 %fusion.10 = f32[256,8,64]{0,2,1:T(8,128)} fusion(bf16[2048,8,64]{0,2,1:T(8,128)(2,1)} %bitcast.83, f32[8,256,2048]{2,1,0:T(8,128)} %copy-done.1, f32[8,256]{1,0:T(8,128)S(1)} %get-tuple-element.249, pred[256,2048]{1,0:T(8,128)(4,1)S(1)} %broadcast_and_fusion), kind=kOutput, calls=%fused_computation.19 | convolution fusion | flops 557842432 | bytes 19931136 | tf_op jit(solution)/shard_map/while/body/eval_jaxpr/hqk,khd->qhd/dot_general | solution.py:60
  82.9 1.5 %copy.28 = f32[256,8,64]{2,1,0:T(8,128)S(1)} copy(f32[256,8,64]{0,2,1:T(8,128)} %fusion.10) | data formatting | bytes 1048576 | tf_op jit(solution)/shard_map/while/body/eval_jaxpr/hqk,khd->qhd/transpose | solution.py:60
  84.4 1.1 reshape.126
  85.5 5.9 %all-to-all-start = ((f32[8,32,512]{2,1,0:T(8,128)}), f32[8,32,512]{2,1,0:T(8,128)}, u32[]{:S(2)}, u32[]{:S(2)}) async-start(f32[8,32,512]{2,1,0:T(8,128)} %reshape.126), calls=%async_computation | async-start | bytes 1048576 | tf_op jit(solution)/shard_map/all_to_all | solution.py:114
  94.0 1.1 reshape.128
  95.1 5.2 %all-gather.4 = f32[4,32,8]{1,2,0:T(8,128)S(1)} all-gather(f32[1,32,8]{1,2,0:T(8,128)S(1)} %bitcast.92), channel_id=3, replica_groups=mesh['region'=8,'tm'=4] {'tm'}, dimensions={0}, use_global_device_ids=true | all-gather | bytes 5120 | tf_op jit(solution)/shard_map/all_gather | solution.py:18
  100.4 5.2 %all-gather.5 = f32[4,32,8]{1,2,0:T(8,128)S(1)} all-gather(f32[1,32,8]{1,2,0:T(8,128)S(1)} %bitcast.90), channel_id=4, replica_groups=mesh['region'=8,'tm'=4] {'tm'}, dimensions={0}, use_global_device_ids=true | all-gather | bytes 5120 | tf_op jit(solution)/shard_map/all_gather | solution.py:18
  105.7 1.3 %multiply_reduce_fusion = f32[32,512]{1,0:T(8,128)S(1)} fusion(f32[8,32,512]{2,1,0:T(8,128)} %all-to-all-done, f32[8,32,512]{2,1,0:T(8,128)} %reshape.128), kind=kLoop, calls=%fused_computation.23 | loop fusion | flops 245760 | bytes 1114112 | tf_op jit(solution)/shard_map/reduce_sum | solution.py:120
  106.9 5.8 %all-gather = f32[128,512]{1,0:T(8,128)S(1)} all-gather(f32[32,512]{1,0:T(8,128)S(1)} %multiply_reduce_fusion), channel_id=2, replica_groups=mesh['region'=8,'tm'=4] {'tm'}, dimensions={0}, use_global_device_ids=true | all-gather | bytes 327680 | tf_op jit(solution)/shard_map/all_gather | solution.py:18
  112.8 1.9 %while.12 = (s32[]{:T(128)}, f32[32,512]{1,0:T(8,128)S(1)}, f32[32,8]{1,0:T(8,128)S(1)}, f32[32,8]{1,0:T(8,128)S(1)}, f32[4,32,8]{1,2,0:T(8,128)S(1)}, /*index=5...) while((s32[]{:T(128)}, f32[32,512]{1,0:T(8,128)S(1)}, ...), condition=%wide.region_8.9_spmd, body=%wide.region_7.8_spmd.sunk | while | flops 50693 | bytes 739479 | solution.py:24
  114.9 1.3 %fusion.54 = (f32[32]{0:T(128)S(1)}, f32[32,512]{1,0:T(8,128)S(1)}) fusion(bf16[512,512]{1,0:T(8,128)(2,1)} %param.21, f32[32,512]{1,0:T(8,128)S(1)} %get-tuple-element.209, f32[32,512]{1,0:T(8,128)S(1)} %reshape.130, bf16[1,32,512]{2,1,0:T(8,128)(2,1)S(1)} %copy-done.2), kind=kOutput, calls=%fused_computation.78 | convolution fusion | flops 16859104 | bytes 753792 | tf_op jit(solution)/shard_map/dot_general | solution.py:124
  116.5 1.6 %fusion.28 = f32[32,512]{1,0:T(8,128)S(1)} fusion(bf16[512,512]{1,0:T(8,128)(2,1)} %param.23, bf16[512,512]{1,0:T(8,128)(2,1)} %param.22, f32[32,512]{1,0:T(8,128)S(1)} %get-tuple-element.252, f32[512]{0:T(512)S(1)} %copy-done.3, f32[32]{0:T(128)S(1)} %add_rsqrt_fusion, f32[32]{0:T(128)S(1)} %broadcast_multiply_fusion), kind=kOutput, calls=%fused_computation.46 | convolution fusion | flops 33767424 | bytes 1181952 | tf_op jit(solution)/shard_map/dot_general | solution.py:129
  118.1 5.9 %all-gather.3 = f32[128,512]{1,0:T(8,128)S(1)} all-gather(f32[32,512]{1,0:T(8,128)S(1)} %fusion.28), channel_id=5, replica_groups=mesh['region'=8,'tm'=4] {'tm'}, dimensions={0}, use_global_device_ids=true | all-gather | bytes 327680 | tf_op jit(solution)/shard_map/all_gather | solution.py:13
  (73 shorter events, 9.5 us)
Async XLA Ops:
  0.0 37.7 %copy-start = (bf16[1,1,2048,512]{3,2,1,0:T(8,128)(2,1)S(1)}, bf16[1,1,2048,512]{3,2,1,0:T(8,128)(2,1)}, u32[]{:S(2)}) copy-start(bf16[1,1,2048,512]{3,2,1,0:T(8,128)(2,1)} %param.13) | copy-start | bytes 6291460
  46.6 5.7 %copy-start.1 = (f32[8,256,2048]{2,1,0:T(8,128)}, f32[8,256,2048]{2,1,0:T(8,128)S(1)}, u32[]{:S(2)}) copy-start(f32[8,256,2048]{2,1,0:T(8,128)S(1)} %get-tuple-element.250) | copy-start | bytes 50331652
  58.1 12.0 %all-to-all-start.2 = ((f32[8,1,256]{2,1,0:T(1,128)}), f32[8,1,256]{2,1,0:T(1,128)S(1)}, u32[]{:S(2)}, u32[]{:S(2)}) async-start(f32[8,1,256]{2,1,0:T(1,128)} %reshape.152), calls=%async_computation.2 | async-start | bytes 16384 | tf_op jit(solution)/shard_map/all_to_all | solution.py:115
  70.1 15.3 %all-to-all-start.1 = ((f32[8,1,256]{2,1,0:T(1,128)}), f32[8,1,256]{2,1,0:T(1,128)S(1)}, u32[]{:S(2)}, u32[]{:S(2)}) async-start(f32[8,1,256]{2,1,0:T(1,128)} %reshape.150), calls=%async_computation.1 | async-start | bytes 16384 | tf_op jit(solution)/shard_map/all_to_all | solution.py:116
  73.5 41.4 %copy-start.2 = (bf16[1,32,512]{2,1,0:T(8,128)(2,1)S(1)}, bf16[1,32,512]{2,1,0:T(8,128)(2,1)}, u32[]{:S(2)}) copy-start(bf16[1,32,512]{2,1,0:T(8,128)(2,1)} %param.16) | copy-start | bytes 98308
  73.5 43.0 %copy-start.3 = (f32[512]{0:T(512)S(1)}, f32[512]{0:T(512)}, u32[]{:S(2)}) copy-start(f32[512]{0:T(512)} %param.18) | copy-start | bytes 6148
  85.5 20.2 %all-to-all-start = ((f32[8,32,512]{2,1,0:T(8,128)}), f32[8,32,512]{2,1,0:T(8,128)}, u32[]{:S(2)}, u32[]{:S(2)}) async-start(f32[8,32,512]{2,1,0:T(8,128)} %reshape.126), calls=%async_computation | async-start | bytes 1048576 | tf_op jit(solution)/shard_map/all_to_all | solution.py:114
